TPU v7x, 32 devices: a whole 2x2x4 slice. The times are simulated.
32 devices in a mesh: rep: 8 (over y, x, core), shard: 4 (over z).
Axes of the slice: x: 2, y: 2, z: 4, core: 2. Of those that a mesh axis runs over, the one named last changes fastest.
Arguments:
- deltas: bfloat16 [8, 512, 4096], P('rep', 'shard'), may hold values from -6 to 6
- presence: int32 [8], replicated, may hold values from 0 to 1, as said below
- owner_of: int32 [8], replicated, may hold values from 0 to 7, each once
- outer_params: float32 [512, 4096], P('shard', 'rep'), may hold values from -6 to 6
- momentum: float32 [512, 4096], P('shard', 'rep'), may hold values from -4 to 4
Outputs:
- new_weights: bfloat16 [512, 4096], P('shard')
- new_outer: float32 [512, 4096], P('shard', 'rep')
- new_momentum: float32 [512, 4096], P('shard', 'rep')
Inputs may be any that keep to these rules, and one draw needn't show every extreme that they name: `presence`: at least one replica group is present.
All inputs are finite; a program needn't handle non-finite values.
Results may differ from a plain program's by a relative error of at most 0.0075.
Values may be sent and summed in bfloat16 or wider, within the bound.
A program may use at most 64 MiB of HBM per device.

v0:
```python
import jax
import jax.numpy as jnp
from jax import lax
from jax.sharding import PartitionSpec as P


def shards(deltas, presence, owner_of, outer_params, momentum):
    groups = lax.axis_size("rep")
    rows = deltas.shape[1]
    width = deltas.shape[2] // groups
    present = presence.astype(jnp.float32)
    count = jnp.sum(present)
    local_blocks = deltas[0].reshape(rows, groups, width)
    slotted = jnp.take(local_blocks, owner_of, axis=1).reshape(rows, groups * width)
    own_flag = lax.dynamic_index_in_dim(present, lax.axis_index("rep"), 0, keepdims=False)
    term = slotted.astype(jnp.float32) * own_flag
    total = lax.psum_scatter(
        term.astype(jnp.bfloat16), "rep", scatter_dimension=1, tiled=True
    ).astype(jnp.float32)
    average = total / count
    new_momentum = 0.9 * momentum + average
    new_outer = outer_params - 0.7 * (average + 0.9 * new_momentum)
    shipped = new_outer.astype(jnp.bfloat16)
    gathered = lax.all_gather(shipped, "rep", axis=1, tiled=True)
    inverse = jnp.argsort(owner_of)
    natural = jnp.take(gathered.reshape(rows, groups, width), inverse, axis=1)
    new_weights = natural.reshape(rows, groups * width)
    return (new_weights, new_outer, new_momentum)


def solution(mesh):
    return jax.shard_map(
        shards,
        mesh=mesh,
        in_specs=(P("rep", "shard", None), P(), P(), P("shard", "rep"), P("shard", "rep")),
        out_specs=(P("shard", None), P("shard", "rep"), P("shard", "rep")),
        check_vma=False,
    )
```

profile of v0, /device:TPU:0, one launch (start us, length us, event | category | flops | bytes accessed | tf_op | source)
XLA Modules:
  0.0 90.7 jit_solution(5586122691734265856)
XLA Ops:
  7.2 0.0 reduce-scatter.2.cloned.1.call-start
  7.2 0.7 compare_select_fusion.1
  7.9 0.7 compare_and_fusion.1
  8.5 0.7 convert_element_type.20
  9.2 1.6 %copy.8 = bf16[1,128,4096]{1,2,0:T(8,128)(2,1)S(1)} copy(bf16[1,128,4096]{2,1,0:T(8,128)(2,1)} %param.7) | data formatting | bytes 2097152 | tf_op args[0]
  10.8 0.5 copy.9
  11.4 0.6 dynamic_slice.4
  12.0 0.6 gather_fusion
  12.6 1.0 %multiply_convert_fusion = bf16[128,8,512]{2,0,1:T(8,128)(2,1)S(1)} fusion(bf16[8,128,512]{2,1,0:T(8,128)(2,1)S(1)} %gather_fusion, f32[]{:T(128)} %bitcast.2, pred[8]{0:T(512)(128)(4,1)S(1)} %compare_and_fusion.1), kind=kLoop, calls=%fused_computation.2 | loop fusion | flops 2097152 | bytes 2097164 | tf_op jit(solution)/shard_map/convert_element_type | solution.py:18
  13.5 1.3 %copy.10 = bf16[128,8,512]{0,2,1:T(8,128)(2,1)} copy(bf16[128,8,512]{2,0,1:T(8,128)(2,1)S(1)} %multiply_convert_fusion) | data formatting | bytes 2097152 | tf_op jit(solution)/shard_map/convert_element_type | solution.py:18
  14.8 0.0 copy-start
  14.9 0.0 copy-start.1
  14.9 0.0 copy-start.2
  14.9 0.0 reduce-scatter.2.cloned.1.call-update
  14.9 0.0 all-gather.2.cloned.1.call-start
  14.9 0.9 copy-done
  15.8 0.1 copy.11
  15.9 0.0 copy-done.1
  15.9 0.0 copy-start.3
  16.0 0.1 copy.12
  16.1 0.0 copy-done.2
  16.1 0.6 convert_reduce_fusion
  16.7 37.1 %reduce-scatter.2.cloned.1.call-done = bf16[128,512]{0,1:T(8,128)(2,1)} async-done(((bf16[128,4096]{0,1:T(8,128)(2,1)}), bf16[128,512]{0,1:T(8,128)(2,1)}) %reduce-scatter.2.cloned.1.call-update) | async-done | bytes 131088 | tf_op jit(solution)/shard_map/reduce_scatter | solution.py:17
  53.7 2.3 %fusion = (bf16[128,512]{0,1:T(8,128)(2,1)}, f32[128,512]{0,1:T(8,128)S(1)}, f32[128,512]{0,1:T(8,128)S(1)}) fusion(f32[128,512]{0,1:T(8,128)S(1)} %copy.12, f32[128,512]{0,1:T(8,128)S(1)} %copy.11, f32[]{:T(128)} %convert_reduce_fusion, bf16[128,512]{0,1:T(8,128)(2,1)} %reduce-scatter.2.cloned.1.call-done), kind=kLoop, calls=%fused_computation.14 | loop fusion | flops 589824 | bytes 1310724 | tf_op jit(solution)/shard_map/convert_element_type | solution.py:23
  56.0 0.0 all-gather.2.cloned.1.call-update
  56.1 0.0 copy-done.3
  56.1 1.0 %sort.17 = (s32[8]{0:T(128)}, s32[8]{0:T(128)S(1)}) sort(s32[8]{0:T(128)S(1)} %copy-done.3, s32[8]{0:T(128)S(1)} %iota.4), dimensions={0}, to_apply=%region_2.4 | sort | flops 24 | bytes 128 | tf_op jit(solution)/shard_map/jit(argsort)/sort | solution.py:25
  57.1 0.8 copy.16
  57.9 0.8 copy.17
  58.7 20.9 %all-gather.2.cloned.1.call-done = bf16[128,4096]{0,1:T(8,128)(2,1)} async-done(((bf16[128,512]{0,1:T(8,128)(2,1)}), bf16[128,4096]{0,1:T(8,128)(2,1)}) %all-gather.2.cloned.1.call-update) | async-done | bytes 1048592 | tf_op jit(solution)/shard_map/all_gather | solution.py:24
  79.6 1.5 %copy.13 = bf16[128,8,512]{2,0,1:T(8,128)(2,1)S(1)} copy(bf16[128,8,512]{0,2,1:T(8,128)(2,1)} %bitcast.12) | data formatting | bytes 2097152 | tf_op jit(solution)/shard_map/reshape | solution.py:26
  81.1 0.6 gather_fusion.1
  81.7 0.2 select_bitcast_fusion
  81.9 0.7 copy.14
  82.6 1.3 %copy.15 = bf16[128,4096]{1,0:T(8,128)(2,1)} copy(bf16[128,4096]{0,1:T(8,128)(2,1)S(1)} %bitcast.10) | data formatting | bytes 2097152
  (5 shorter events, 0.0 us)
Async XLA Ops:
  7.2 46.6 %reduce-scatter.2.cloned.1.call-start = ((), (), s32[]{:S(2)}) async-start(), calls=%async_computation.1 | async-start | bytes 1179648 | tf_op jit(solution)/shard_map/reduce_scatter | solution.py:17
  14.8 0.9 %copy-start = (f32[128,512]{1,0:T(8,128)S(1)}, f32[128,512]{1,0:T(8,128)}, u32[]{:S(2)}) copy-start(f32[128,512]{1,0:T(8,128)} %param.11) | copy-start | bytes 786436
  14.9 1.1 %copy-start.1 = (f32[128,512]{1,0:T(8,128)S(1)}, f32[128,512]{1,0:T(8,128)}, u32[]{:S(2)}) copy-start(f32[128,512]{1,0:T(8,128)} %param.10) | copy-start | bytes 786436
  14.9 1.2 %copy-start.2 = (s32[8]{0:T(128)S(1)}, s32[8]{0:T(128)}, u32[]{:S(2)}) copy-start(s32[8]{0:T(128)} %param.8) | copy-start | bytes 100
  14.9 64.7 %all-gather.2.cloned.1.call-start = ((), (), s32[]{:S(2)}) async-start(), calls=%async_computation.2 | async-start | bytes 1179648 | tf_op jit(solution)/shard_map/all_gather | solution.py:24
  15.9 40.1 %copy-start.3 = (s32[8]{0:T(128)S(1)}, s32[8]{0:T(128)}, u32[]{:S(2)}) copy-start(s32[8]{0:T(128)} %param.9) | copy-start | bytes 100
Sparse Core Ops, SparseCore 0:
  15.0 38.6 reduce-scatter.1
  56.2 23.3 all-gather.1
where the time goes:
time: 91 us; the launch traced here: 90.7 us
  waiting for transfers between devices  58 us (64%)
  between operations  14.2 us (16%)
  local copies, waits for them, and re-layouts  11.5 us (13%)
  other arithmetic  6.97 us (8%)
    reduce_scatter x1, waiting for transfers between devices, shards(): lax.psum_scatter(term.astype(jnp.bfloat16), 'rep', scatter_dimension=1, t...  37.1 us
    all_gather x1, waiting for transfers between devices, shards(): gathered = lax.all_gather(shipped, 'rep', axis=1, tiled=True)  20.9 us
    unnamed x14, local copies, waits for them, and re-layouts  5.72 us
    convert_element_type x1, other arithmetic, shards(): shipped = new_outer.astype(jnp.bfloat16)  2.29 us
  transfers between devices with their start and end apart: 2, of which 2 were waited for; matrix products, arithmetic and copies ran while one was open for 4% of the time, Pallas kernels for 0%

commit v1 on v0

v1 whole, which is shorter than its diff:
```python
import functools

import jax
import jax.numpy as jnp
from jax import lax
from jax.experimental import pallas as pl
from jax.experimental.pallas import tpu as pltpu
from jax.sharding import PartitionSpec as P

MESH = pl.DeviceIdType.MESH


def toggled(index, mask, size):
    out, bit = 0, 1
    while bit < size:
        digit = (index // bit) % 2
        out = out + bit * ((1 - digit) if mask & bit else digit)
        bit *= 2
    return out


def exchange(n, chunks, presence, owner_of, deltas, outer_params, momentum, gathered, average,
             held_low, held_high, params, speed, out0, in0, out1, own, in1,
             load_sem, state_sem, send0, recv0, send1, recv1, send2, recv2, send3, recv3):
    me = lax.axis_index("rep")
    side, team = me % 2, me // 2
    partner = me + 1 - 2 * side
    teams = n // 2
    rows, width = average.shape
    part = rows // chunks
    mates = [toggled(team, d, teams) for d in range(teams)]
    peers = [2 * mate + side for mate in mates]
    order = list(range(teams - 1, 0, -1))

    def span(k):
        return pl.ds(k * part, part)

    def remote(src, dst, send, recv, to):
        return pltpu.make_async_remote_copy(
            src_ref=src, dst_ref=dst, send_sem=send, recv_sem=recv, device_id={"rep": to}, device_id_type=MESH)

    barrier = pltpu.get_barrier_semaphore()
    for to in [partner] + [peers[d] for d in order]:
        pl.semaphore_signal(barrier, inc=1, device_id={"rep": to}, device_id_type=MESH)

    held = (held_low, held_high)
    pieces, tall = len(held), rows // len(held)
    loads = [[pltpu.make_async_copy(deltas.at[0, pl.ds(i * tall, tall), pl.ds(j * width, width)],
                                    held[i].at[j], load_sem.at[i, j]) for j in range(n)]
             for i in range(pieces)]
    for load in sum(loads, []):
        load.start()
    state = [pltpu.make_async_copy(outer_params, params, state_sem.at[0]),
             pltpu.make_async_copy(momentum, speed, state_sem.at[1])]
    for load in state:
        load.start()

    flag = presence[me].astype(jnp.float32)
    count = presence[0].astype(jnp.float32)
    for r in range(1, n):
        count = count + presence[r].astype(jnp.float32)
    share = jnp.full((1, width), 1.0, jnp.float32) / jnp.full((1, width), count, jnp.float32)

    def term(k, slot):
        piece, first = divmod(k * part, tall)
        return held[piece][owner_of[slot], pl.ds(first, part)].astype(jnp.float32) * flag

    pending = []
    for k in range(chunks):
        if (k * part) % tall == 0:
            for load in loads[k * part // tall]:
                load.wait()
        for d in range(teams):
            out0[k, d] = term(k, 2 * mates[d] + 1 - side).astype(jnp.bfloat16)
        if k == 0:
            pl.semaphore_wait(barrier, teams)
        copy = remote(out0.at[k], in0.at[k], send0.at[k], recv0.at[k], partner)
        copy.start()
        pending.append(copy)
    firsts = list(pending)

    seconds = {}
    for k in range(chunks):
        firsts[k].wait_recv()
        for d in order:
            total = term(k, peers[d]) + in0[k, d].astype(jnp.float32)
            out1[k, d - 1] = total.astype(jnp.bfloat16)
            copy = remote(out1.at[k, d - 1], in1.at[k, d - 1], send1.at[k, d - 1], recv1.at[k, d - 1], peers[d])
            copy.start()
            seconds[k, d] = copy
            pending.append(copy)
        own[span(k)] = term(k, peers[0]) + in0[k, 0].astype(jnp.float32)

    for load in state:
        load.wait()
    thirds, fourths = {}, []
    for k in range(chunks):
        total = own[span(k)]
        for d in order:
            seconds[k, d].wait_recv()
            total = total + in1[k, d - 1].astype(jnp.float32)
        mean = total * share
        average[span(k)] = mean
        new_momentum = 0.9 * speed[span(k)] + mean
        new_outer = params[span(k)] - 0.7 * (mean + 0.9 * new_momentum)
        gathered[me, span(k)] = new_outer.astype(jnp.bfloat16)
        block = gathered.at[me, span(k)]
        for d in order:
            copy = remote(block, block, send2.at[k, d - 1], recv2.at[k, d - 1], peers[d])
            copy.start()
            thirds[k, d] = copy
            pending.append(copy)
        copy = remote(block, block, send3.at[k, 0], recv3.at[k, 0], partner)
        copy.start()
        fourths.append(copy)

    for k in range(chunks):
        for d in order[::-1]:
            thirds[k, d].wait_recv()
            block = gathered.at[peers[d], span(k)]
            copy = remote(block, block, send3.at[k, d], recv3.at[k, d], partner)
            copy.start()
            fourths.append(copy)
    for copy in fourths:
        copy.wait_recv()
    for copy in pending + fourths:
        copy.wait_send()


def finish(n, owner_of, gathered, average, outer_params, momentum, new_weights, new_outer, new_momentum,
           outer_out, momentum_out, block_sem, state_sem):
    width = gathered.shape[2]
    copies = []
    for j in range(n):
        start = pl.multiple_of(owner_of[j] * width, width)
        copies.append(pltpu.make_async_copy(gathered.at[j], new_weights.at[:, pl.ds(start, width)], block_sem.at[j]))
    for copy in copies:
        copy.start()
    mean = average[...]
    speed = 0.9 * momentum[...] + mean
    momentum_out[...] = speed
    outer_out[...] = outer_params[...] - 0.7 * (mean + 0.9 * speed)
    last = [pltpu.make_async_copy(momentum_out, new_momentum, state_sem.at[0]),
            pltpu.make_async_copy(outer_out, new_outer, state_sem.at[1])]
    for copy in last:
        copy.start()
    for copy in copies + last:
        copy.wait()


def shards(deltas, presence, owner_of, outer_params, momentum):
    n = lax.axis_size("rep")
    teams = n // 2
    rows, width = outer_params.shape
    chunks = 4
    part = rows // chunks
    bf16, f32 = jnp.bfloat16, jnp.float32
    smem = pl.BlockSpec(memory_space=pltpu.SMEM)
    vmem = pl.BlockSpec(memory_space=pltpu.VMEM)
    anywhere = pl.BlockSpec(memory_space=pl.ANY)
    hbm = pl.BlockSpec(memory_space=pltpu.HBM)
    dma = pltpu.SemaphoreType.DMA
    gathered, average = pl.pallas_call(
        functools.partial(exchange, n, chunks),
        out_shape=(jax.ShapeDtypeStruct((n, rows, width), bf16), jax.ShapeDtypeStruct((rows, width), f32)),
        in_specs=[smem, smem, hbm, hbm, hbm],
        out_specs=(vmem, vmem),
        scratch_shapes=[
            pltpu.VMEM((n, rows // 2, width), bf16),
            pltpu.VMEM((n, rows // 2, width), bf16),
            pltpu.VMEM((rows, width), f32),
            pltpu.VMEM((rows, width), f32),
            pltpu.VMEM((chunks, teams, part, width), bf16),
            pltpu.VMEM((chunks, teams, part, width), bf16),
            pltpu.VMEM((chunks, teams - 1, part, width), bf16),
            pltpu.VMEM((rows, width), f32),
            pltpu.VMEM((chunks, teams - 1, part, width), bf16),
            dma((2, n)), dma((2,)),
            dma((chunks,)), dma((chunks,)),
            dma((chunks, teams - 1)), dma((chunks, teams - 1)),
            dma((chunks, teams - 1)), dma((chunks, teams - 1)),
            dma((chunks, teams)), dma((chunks, teams)),
        ],
        compiler_params=pltpu.CompilerParams(collective_id=0, has_side_effects=True, vmem_limit_bytes=12 << 20),
        name="exchange",
    )(presence, owner_of, deltas, outer_params, momentum)
    return pl.pallas_call(
        functools.partial(finish, n),
        out_shape=(
            jax.ShapeDtypeStruct((rows, n * width), bf16),
            jax.ShapeDtypeStruct((rows, width), f32),
            jax.ShapeDtypeStruct((rows, width), f32),
        ),
        in_specs=[smem, vmem, vmem, vmem, vmem],
        out_specs=(anywhere, anywhere, anywhere),
        scratch_shapes=[
            pltpu.VMEM((rows, width), f32),
            pltpu.VMEM((rows, width), f32),
            dma((n,)), dma((2,)),
        ],
        compiler_params=pltpu.CompilerParams(vmem_limit_bytes=8 << 20),
        name="finish",
    )(owner_of, gathered, average, outer_params, momentum)


def solution(mesh):
    return jax.shard_map(
        shards,
        mesh=mesh,
        in_specs=(P("rep", "shard", None), P(), P(), P("shard", "rep"), P("shard", "rep")),
        out_specs=(P("shard", None), P("shard", "rep"), P("shard", "rep")),
        check_vma=False,
    )
```

time: 91 us -> 27 us (0.30)
  waiting for transfers between devices: 58 us -> 0 us
  Pallas kernels: 0 us -> 21.7 us
  between operations: 14.2 us -> 0.65 us
  local copies, waits for them, and re-layouts: 11.5 us -> 4.43 us
  other arithmetic: 6.97 us -> 0 us
    reduce_scatter x1 -> x0, waiting for transfers between devices: 37.1 us -> none  [shards(): lax.psum_scatter(term.astype(jnp.bfloat16), 'rep', scatter_dimension=1, t...]
    pallas_call x0 -> x2, Pallas kernels: none -> 21.7 us  [the longest x1 19.9 us: shards(): pl.pallas_call(functools.partial(exchange, n, chunks), out_shape=(jax.Sha...]
    all_gather x1 -> x0, waiting for transfers between devices: 20.9 us -> none  [shards(): gathered = lax.all_gather(shipped, 'rep', axis=1, tiled=True)]
    convert_element_type x3 -> x0, other arithmetic: 3.9 us -> none  [the longest x1 2.29 us: shards(): shipped = new_outer.astype(jnp.bfloat16)]
    reshape x1 -> x0, local copies, waits for them, and re-layouts: 1.48 us -> none  [shards(): natural = jnp.take(gathered.reshape(rows, groups, width), inverse, axis=1)]
    convert_element_type x1 -> x0, local copies, waits for them, and re-layouts: 1.31 us -> none  [shards(): term.astype(jnp.bfloat16)]
    unnamed x14 -> x10, local copies, waits for them, and re-layouts: 5.72 us -> 4.43 us
    gather x2 -> x0, local copies, waits for them, and re-layouts: 1.23 us -> none  [the longest x1 0.61 us: shards(): natural = jnp.take(gathered.reshape(rows, groups, width), inverse, axis=1)]
  transfers between devices with their start and end apart: 2 -> 0, of which waited for: 2 -> 0; matrix products, arithmetic and copies ran while one was open for 4% -> 0% of each run, Pallas kernels for 0% -> 0%
where the time goes in v1:
time: 27 us; the launch traced here: 26.8 us
  Pallas kernels  21.7 us (80%)
  local copies, waits for them, and re-layouts  4.43 us (16%)
  between operations  0.65 us (2%)
    pallas_call x1, Pallas kernels, shards(): pl.pallas_call(functools.partial(exchange, n, chunks), out_shape=(jax.Sha...  19.9 us
    unnamed x10, local copies, waits for them, and re-layouts  4.43 us
    pallas_call x1, Pallas kernels, shards(): pl.pallas_call(functools.partial(finish, n), out_shape=(jax.ShapeDtypeStr...  1.77 us

profile of v1, /device:TPU:0, one launch (start us, length us, event | category | flops | bytes accessed | tf_op | source)
XLA Modules:
  0.0 26.8 jit_solution(15354600039698482223)
XLA Ops:
  0.6 0.0 copy-start
  0.6 1.2 %copy-done = bf16[1,128,4096]{2,1,0:T(8,128)(2,1)S(1)} copy-done((bf16[1,128,4096]{2,1,0:T(8,128)(2,1)S(1)}, bf16[1,128,4096]{2,1,0:T(8,128)(2,1)}, u32[]{:S(2)}) %copy-start) | copy-done | bytes 1048600
  1.9 0.0 copy-start.1
  1.9 0.9 %copy-done.1 = f32[128,512]{1,0:T(8,128)S(1)} copy-done((f32[128,512]{1,0:T(8,128)S(1)}, f32[128,512]{1,0:T(8,128)}, u32[]{:S(2)}) %copy-start.1) | copy-done | bytes 262168
  2.8 0.0 copy-start.2
  2.8 0.9 %copy-done.2 = f32[128,512]{1,0:T(8,128)S(1)} copy-done((f32[128,512]{1,0:T(8,128)S(1)}, f32[128,512]{1,0:T(8,128)}, u32[]{:S(2)}) %copy-start.2) | copy-done | bytes 262168
  3.8 0.0 copy-start.3
  3.8 0.7 %copy-done.3 = s32[8]{0:T(128)S(1)} copy-done((s32[8]{0:T(128)S(1)}, s32[8]{0:T(128)}, u32[]{:S(2)}) %copy-start.3) | copy-done | bytes 56
  4.4 0.0 copy-start.4
  4.4 0.7 %copy-done.4 = s32[8]{0:T(128)S(1)} copy-done((s32[8]{0:T(128)S(1)}, s32[8]{0:T(128)}, u32[]{:S(2)}) %copy-start.4) | copy-done | bytes 56
  5.1 19.9 %exchange.1 = (bf16[8,128,512]{2,1,0:T(8,128)(2,1)S(1)}, f32[128,512]{1,0:T(8,128)S(1)}) custom-call(s32[8]{0:T(128)S(1)} %copy-done.4, s32[8]{0:T(128)S(1)} %copy-done.3, bf16[1,128,4096]{2,1,0:T(8,128)(2,1)S(1)} %copy-done, f32[128,512]{1,0:T(8,128)S(1)} %copy-done.1, f32[128,512]{1,0:T(8,128)S(1)} %copy-done.2), custom_call_target="tpu_custom_call" | custom-call | tf_op jit(solution)/shard_map/exchange/pallas_call | solution.py:163
  25.0 1.8 %finish.1 = (bf16[128,4096]{1,0:T(8,128)(2,1)}, f32[128,512]{1,0:T(8,128)}, f32[128,512]{1,0:T(8,128)}) custom-call(s32[8]{0:T(128)S(1)} %copy-done.3, bf16[8,128,512]{2,1,0:T(8,128)(2,1)S(1)} %get-tuple-element.5.gathered, f32[128,512]{1,0:T(8,128)S(1)} %get-tuple-element.6.average, f32[128,512]{1,0:T(8,128)S(1)} %copy-done.1, f32[128,512]{1,0:T(8,128)S(1)} %copy-done.2), custom_call_target="tpu_custom_call" | custom-call | tf_op jit(solution)/shard_map/finish/pallas_call | solution.py:187
Async XLA Ops:
  0.6 1.2 %copy-start = (bf16[1,128,4096]{2,1,0:T(8,128)(2,1)S(1)}, bf16[1,128,4096]{2,1,0:T(8,128)(2,1)}, u32[]{:S(2)}) copy-start(bf16[1,128,4096]{2,1,0:T(8,128)(2,1)} %deltas.1) | copy-start | bytes 3145732
  1.9 0.9 %copy-start.1 = (f32[128,512]{1,0:T(8,128)S(1)}, f32[128,512]{1,0:T(8,128)}, u32[]{:S(2)}) copy-start(f32[128,512]{1,0:T(8,128)} %outer_params.3) | copy-start | bytes 786436
  2.8 0.9 %copy-start.2 = (f32[128,512]{1,0:T(8,128)S(1)}, f32[128,512]{1,0:T(8,128)}, u32[]{:S(2)}) copy-start(f32[128,512]{1,0:T(8,128)} %momentum.3) | copy-start | bytes 786436
  3.8 0.7 %copy-start.3 = (s32[8]{0:T(128)S(1)}, s32[8]{0:T(128)}, u32[]{:S(2)}) copy-start(s32[8]{0:T(128)} %owner_of.3) | copy-start | bytes 100
  4.4 0.7 %copy-start.4 = (s32[8]{0:T(128)S(1)}, s32[8]{0:T(128)}, u32[]{:S(2)}) copy-start(s32[8]{0:T(128)} %presence.1) | copy-start | bytes 100

commit v2 on v1

--- a/solution.py
+++ b/solution.py
@@ -19,14 +19,14 @@
     return out
 
 
-def exchange(n, chunks, presence, owner_of, deltas, outer_params, momentum, gathered, average,
+def exchange(n, chunks, presence, owner_of, deltas, outer_params, momentum, gathered, outer_out, momentum_out,
              held_low, held_high, params, speed, out0, in0, out1, own, in1,
              load_sem, state_sem, send0, recv0, send1, recv1, send2, recv2, send3, recv3):
     me = lax.axis_index("rep")
     side, team = me % 2, me // 2
     partner = me + 1 - 2 * side
     teams = n // 2
-    rows, width = average.shape
+    rows, width = outer_out.shape
     part = rows // chunks
     mates = [toggled(team, d, teams) for d in range(teams)]
     peers = [2 * mate + side for mate in mates]
@@ -100,9 +100,10 @@
             seconds[k, d].wait_recv()
             total = total + in1[k, d - 1].astype(jnp.float32)
         mean = total * share
-        average[span(k)] = mean
         new_momentum = 0.9 * speed[span(k)] + mean
         new_outer = params[span(k)] - 0.7 * (mean + 0.9 * new_momentum)
+        momentum_out[span(k)] = new_momentum
+        outer_out[span(k)] = new_outer
         gathered[me, span(k)] = new_outer.astype(jnp.bfloat16)
         block = gathered.at[me, span(k)]
         for d in order:
@@ -127,24 +128,17 @@
         copy.wait_send()
 
 
-def finish(n, owner_of, gathered, average, outer_params, momentum, new_weights, new_outer, new_momentum,
-           outer_out, momentum_out, block_sem, state_sem):
+def finish(n, owner_of, gathered, outer, speed, new_weights, new_outer, new_momentum, block_sem, state_sem):
     width = gathered.shape[2]
     copies = []
     for j in range(n):
         start = pl.multiple_of(owner_of[j] * width, width)
         copies.append(pltpu.make_async_copy(gathered.at[j], new_weights.at[:, pl.ds(start, width)], block_sem.at[j]))
+    copies += [pltpu.make_async_copy(outer, new_outer, state_sem.at[0]),
+               pltpu.make_async_copy(speed, new_momentum, state_sem.at[1])]
     for copy in copies:
         copy.start()
-    mean = average[...]
-    speed = 0.9 * momentum[...] + mean
-    momentum_out[...] = speed
-    outer_out[...] = outer_params[...] - 0.7 * (mean + 0.9 * speed)
-    last = [pltpu.make_async_copy(momentum_out, new_momentum, state_sem.at[0]),
-            pltpu.make_async_copy(outer_out, new_outer, state_sem.at[1])]
-    for copy in last:
-        copy.start()
-    for copy in copies + last:
+    for copy in copies:
         copy.wait()
 
 
@@ -160,11 +154,13 @@
     anywhere = pl.BlockSpec(memory_space=pl.ANY)
     hbm = pl.BlockSpec(memory_space=pltpu.HBM)
     dma = pltpu.SemaphoreType.DMA
-    gathered, average = pl.pallas_call(
+    here = functools.partial(pltpu.with_memory_space_constraint, memory_space=pltpu.HBM)
+    owner_of = here(owner_of)
+    gathered, outer, speed = pl.pallas_call(
         functools.partial(exchange, n, chunks),
-        out_shape=(jax.ShapeDtypeStruct((n, rows, width), bf16), jax.ShapeDtypeStruct((rows, width), f32)),
+        out_shape=(pltpu.VMEM((n, rows, width), bf16), pltpu.VMEM((rows, width), f32), pltpu.VMEM((rows, width), f32)),
         in_specs=[smem, smem, hbm, hbm, hbm],
-        out_specs=(vmem, vmem),
+        out_specs=(vmem, vmem, vmem),
         scratch_shapes=[
             pltpu.VMEM((n, rows // 2, width), bf16),
             pltpu.VMEM((n, rows // 2, width), bf16),
@@ -183,7 +179,7 @@
         ],
         compiler_params=pltpu.CompilerParams(collective_id=0, has_side_effects=True, vmem_limit_bytes=12 << 20),
         name="exchange",
-    )(presence, owner_of, deltas, outer_params, momentum)
+    )(here(presence), owner_of, here(deltas), here(outer_params), here(momentum))
     return pl.pallas_call(
         functools.partial(finish, n),
         out_shape=(
@@ -191,16 +187,12 @@
             jax.ShapeDtypeStruct((rows, width), f32),
             jax.ShapeDtypeStruct((rows, width), f32),
         ),
-        in_specs=[smem, vmem, vmem, vmem, vmem],
+        in_specs=[smem, vmem, vmem, vmem],
         out_specs=(anywhere, anywhere, anywhere),
-        scratch_shapes=[
-            pltpu.VMEM((rows, width), f32),
-            pltpu.VMEM((rows, width), f32),
-            dma((n,)), dma((2,)),
-        ],
+        scratch_shapes=[dma((n,)), dma((2,))],
         compiler_params=pltpu.CompilerParams(vmem_limit_bytes=8 << 20),
         name="finish",
-    )(owner_of, gathered, average, outer_params, momentum)
+    )(owner_of, gathered, outer, speed)
 
 
 def solution(mesh):

time: 27 us -> 23 us (0.85)
  local copies, waits for them, and re-layouts: 4.43 us -> 0 us
  Pallas kernels: 21.7 us -> 22.2 us
    unnamed x10 -> x0, local copies, waits for them, and re-layouts: 4.43 us -> none
    pallas_call x1, Pallas kernels: 19.9 us -> 20.3 us  [shards(): pl.pallas_call(functools.partial(exchange, n, chunks), out_shape=(pltpu.V...]
where the time goes in v2:
time: 23 us; the launch traced here: 22.9 us
  Pallas kernels  22.2 us (97%)
  between operations  0.64 us (3%)
    pallas_call x1, Pallas kernels, shards(): pl.pallas_call(functools.partial(exchange, n, chunks), out_shape=(pltpu.V...  20.3 us
    pallas_call x1, Pallas kernels, shards(): pl.pallas_call(functools.partial(finish, n), out_shape=(jax.ShapeDtypeStr...  1.89 us

profile of v2, /device:TPU:0, one launch (start us, length us, event | category | flops | bytes accessed | tf_op | source)
XLA Modules:
  0.0 22.9 jit_solution(12671681686462344667)
XLA Ops:
  0.6 20.3 %exchange.1 = (bf16[8,128,512]{2,1,0:T(8,128)(2,1)S(1)}, f32[128,512]{1,0:T(8,128)S(1)}, f32[128,512]{1,0:T(8,128)S(1)}) custom-call(s32[8]{0:T(128)} %presence.1, s32[8]{0:T(128)} %owner_of.3, bf16[1,128,4096]{2,1,0:T(8,128)(2,1)} %deltas.1, f32[128,512]{1,0:T(8,128)} %outer_params.1, f32[128,512]{1,0:T(8,128)} %momentum.1), custom_call_target="tpu_custom_call" | custom-call | tf_op jit(solution)/shard_map/exchange/pallas_call | solution.py:159
  21.0 1.9 %finish.1 = (bf16[128,4096]{1,0:T(8,128)(2,1)}, f32[128,512]{1,0:T(8,128)}, f32[128,512]{1,0:T(8,128)}) custom-call(s32[8]{0:T(128)} %owner_of.3, bf16[8,128,512]{2,1,0:T(8,128)(2,1)S(1)} %get-tuple-element.6.gathered, f32[128,512]{1,0:T(8,128)S(1)} %get-tuple-element.7.outer, f32[128,512]{1,0:T(8,128)S(1)} %get-tuple-element.8.speed), custom_call_target="tpu_custom_call" | custom-call | tf_op jit(solution)/shard_map/finish/pallas_call | solution.py:183

commit v3 on v2

--- a/solution.py
+++ b/solution.py
@@ -20,8 +20,8 @@
 
 
 def exchange(n, chunks, presence, owner_of, deltas, outer_params, momentum, gathered, outer_out, momentum_out,
-             held_low, held_high, params, speed, out0, in0, out1, own, in1,
-             load_sem, state_sem, send0, recv0, send1, recv1, send2, recv2, send3, recv3):
+             held_low, held_high, params, speed, out0, in0, out1, in1, out2, in2, own,
+             load_sem, state_sem, send0, recv0, send1, recv1, send2, recv2, send3, recv3, send4, recv4):
     me = lax.axis_index("rep")
     side, team = me % 2, me // 2
     partner = me + 1 - 2 * side
@@ -79,52 +79,111 @@
         pending.append(copy)
     firsts = list(pending)
 
+    low = 1
+    while low * low * 4 <= teams:
+        low *= 2
+    plans = []
+    for k in range(chunks):
+        steps = (1, low) if k % 2 == 0 else (low, 1)
+        sizes = (low, teams // low) if k % 2 == 0 else (teams // low, low)
+        plans.append((sizes, lambda f, s, steps=steps: f * steps[0] + s * steps[1]))
+
+    def pair_sum(k, d):
+        return term(k, peers[d]) + in0[k, d].astype(jnp.float32)
+
     seconds = {}
     for k in range(chunks):
+        (first, second), mask = plans[k]
         firsts[k].wait_recv()
-        for d in order:
-            total = term(k, peers[d]) + in0[k, d].astype(jnp.float32)
-            out1[k, d - 1] = total.astype(jnp.bfloat16)
-            copy = remote(out1.at[k, d - 1], in1.at[k, d - 1], send1.at[k, d - 1], recv1.at[k, d - 1], peers[d])
+        for f in range(1, first):
+            for s in range(second):
+                out1[k, (f - 1) * second + s] = pair_sum(k, mask(f, s)).astype(jnp.bfloat16)
+            bundle = pl.ds((f - 1) * second, second)
+            copy = remote(out1.at[k, bundle], in1.at[k, bundle], send1.at[k, f - 1], recv1.at[k, f - 1],
+                          peers[mask(f, 0)])
             copy.start()
-            seconds[k, d] = copy
+            seconds[k, f] = copy
             pending.append(copy)
-        own[span(k)] = term(k, peers[0]) + in0[k, 0].astype(jnp.float32)
+
+    thirds = {}
+    for k in range(chunks):
+        (first, second), mask = plans[k]
+        for f in range(1, first):
+            seconds[k, f].wait_recv()
+        for s in list(range(1, second)) + [0]:
+            total = pair_sum(k, mask(0, s))
+            for f in range(1, first):
+                total = total + in1[k, (f - 1) * second + s].astype(jnp.float32)
+            if s == 0:
+                own[span(k)] = total
+                continue
+            out2[k, s - 1] = total.astype(jnp.bfloat16)
+            copy = remote(out2.at[k, s - 1], in2.at[k, s - 1], send2.at[k, s - 1], recv2.at[k, s - 1],
+                          peers[mask(0, s)])
+            copy.start()
+            thirds[k, s] = copy
+            pending.append(copy)
 
     for load in state:
         load.wait()
-    thirds, fourths = {}, []
-    for k in range(chunks):
+    arrivals, handed = {}, []
+
+    def ship(k, origin, via):
+        block, d = gathered.at[peers[origin], span(k)], origin + via
+        arrivals[k, d] = remote(block, block, send3.at[k, d - 1], recv3.at[k, d - 1], peers[via])
+        arrivals[k, d].start()
+        pending.append(arrivals[k, d])
+
+    def hand(k, d):
+        block = gathered.at[peers[d], span(k)]
+        copy = remote(block, block, send4.at[k, d], recv4.at[k, d], partner)
+        copy.start()
+        handed.append(copy)
+
+    def update(k):
+        (first, second), mask = plans[k]
         total = own[span(k)]
-        for d in order:
-            seconds[k, d].wait_recv()
-            total = total + in1[k, d - 1].astype(jnp.float32)
+        for s in range(1, second):
+            thirds[k, s].wait_recv()
+            total = total + in2[k, s - 1].astype(jnp.float32)
         mean = total * share
         new_momentum = 0.9 * speed[span(k)] + mean
         new_outer = params[span(k)] - 0.7 * (mean + 0.9 * new_momentum)
+        gathered[me, span(k)] = new_outer.astype(jnp.bfloat16)
+        for f in range(1, first):
+            ship(k, 0, mask(f, 0))
+        for s in range(1, second):
+            ship(k, 0, mask(0, s))
+        hand(k, 0)
         momentum_out[span(k)] = new_momentum
         outer_out[span(k)] = new_outer
-        gathered[me, span(k)] = new_outer.astype(jnp.bfloat16)
-        block = gathered.at[me, span(k)]
-        for d in order:
-            copy = remote(block, block, send2.at[k, d - 1], recv2.at[k, d - 1], peers[d])
-            copy.start()
-            thirds[k, d] = copy
-            pending.append(copy)
-        copy = remote(block, block, send3.at[k, 0], recv3.at[k, 0], partner)
-        copy.start()
-        fourths.append(copy)
-
-    for k in range(chunks):
-        for d in order[::-1]:
-            thirds[k, d].wait_recv()
-            block = gathered.at[peers[d], span(k)]
-            copy = remote(block, block, send3.at[k, d], recv3.at[k, d], partner)
-            copy.start()
-            fourths.append(copy)
-    for copy in fourths:
+
+    def relay(k):
+        (first, second), mask = plans[k]
+        for f in range(1, first):
+            arrivals[k, mask(f, 0)].wait_recv()
+            for s in range(1, second):
+                ship(k, mask(f, 0), mask(0, s))
+            hand(k, mask(f, 0))
+
+    def settle(k):
+        (first, second), mask = plans[k]
+        for s in range(1, second):
+            for f in range(first):
+                arrivals[k, mask(f, s)].wait_recv()
+                hand(k, mask(f, s))
+
+    lag = min(2, chunks)
+    for k in range(chunks + lag):
+        if k < chunks:
+            update(k)
+        if k >= lag:
+            relay(k - lag)
+    for k in range(chunks):
+        settle(k)
+    for copy in handed:
         copy.wait_recv()
-    for copy in pending + fourths:
+    for copy in pending + handed:
         copy.wait_send()
 
 
@@ -169,10 +228,13 @@
             pltpu.VMEM((chunks, teams, part, width), bf16),
             pltpu.VMEM((chunks, teams, part, width), bf16),
             pltpu.VMEM((chunks, teams - 1, part, width), bf16),
+            pltpu.VMEM((chunks, teams - 1, part, width), bf16),
+            pltpu.VMEM((chunks, teams - 1, part, width), bf16),
+            pltpu.VMEM((chunks, teams - 1, part, width), bf16),
             pltpu.VMEM((rows, width), f32),
-            pltpu.VMEM((chunks, teams - 1, part, width), bf16),
             dma((2, n)), dma((2,)),
             dma((chunks,)), dma((chunks,)),
+            dma((chunks, teams - 1)), dma((chunks, teams - 1)),
             dma((chunks, teams - 1)), dma((chunks, teams - 1)),
             dma((chunks, teams - 1)), dma((chunks, teams - 1)),
             dma((chunks, teams)), dma((chunks, teams)),

time: 23 us -> 25.7 us (1.12)
  Pallas kernels: 22.2 us -> 24.9 us
    pallas_call x1, Pallas kernels: 20.3 us -> 23 us  [shards(): pl.pallas_call(functools.partial(exchange, n, chunks), out_shape=(pltpu.V...]
where the time goes in v3:
time: 25.7 us; the launch traced here: 25.5 us
  Pallas kernels  24.9 us (97%)
  between operations  0.64 us (2%)
    pallas_call x1, Pallas kernels, shards(): pl.pallas_call(functools.partial(exchange, n, chunks), out_shape=(pltpu.V...  23 us
    pallas_call x1, Pallas kernels, shards(): pl.pallas_call(functools.partial(finish, n), out_shape=(jax.ShapeDtypeStr...  1.89 us

profile of v3, /device:TPU:0, one launch (start us, length us, event | category | flops | bytes accessed | tf_op | source)
XLA Modules:
  0.0 25.5 jit_solution(12305410364345831125)
XLA Ops:
  0.6 23.0 %exchange.1 = (bf16[8,128,512]{2,1,0:T(8,128)(2,1)S(1)}, f32[128,512]{1,0:T(8,128)S(1)}, f32[128,512]{1,0:T(8,128)S(1)}) custom-call(s32[8]{0:T(128)} %presence.1, s32[8]{0:T(128)} %owner_of.3, bf16[1,128,4096]{2,1,0:T(8,128)(2,1)} %deltas.1, f32[128,512]{1,0:T(8,128)} %outer_params.1, f32[128,512]{1,0:T(8,128)} %momentum.1), custom_call_target="tpu_custom_call" | custom-call | tf_op jit(solution)/shard_map/exchange/pallas_call | solution.py:218
  23.6 1.9 %finish.1 = (bf16[128,4096]{1,0:T(8,128)(2,1)}, f32[128,512]{1,0:T(8,128)}, f32[128,512]{1,0:T(8,128)}) custom-call(s32[8]{0:T(128)} %owner_of.3, bf16[8,128,512]{2,1,0:T(8,128)(2,1)S(1)} %get-tuple-element.6.gathered, f32[128,512]{1,0:T(8,128)S(1)} %get-tuple-element.7.outer, f32[128,512]{1,0:T(8,128)S(1)} %get-tuple-element.8.speed), custom_call_target="tpu_custom_call" | custom-call | tf_op jit(solution)/shard_map/finish/pallas_call | solution.py:245

commit v4 on v2

--- a/solution.py
+++ b/solution.py
@@ -39,10 +39,6 @@
         return pltpu.make_async_remote_copy(
             src_ref=src, dst_ref=dst, send_sem=send, recv_sem=recv, device_id={"rep": to}, device_id_type=MESH)
 
-    barrier = pltpu.get_barrier_semaphore()
-    for to in [partner] + [peers[d] for d in order]:
-        pl.semaphore_signal(barrier, inc=1, device_id={"rep": to}, device_id_type=MESH)
-
     held = (held_low, held_high)
     pieces, tall = len(held), rows // len(held)
     loads = [[pltpu.make_async_copy(deltas.at[0, pl.ds(i * tall, tall), pl.ds(j * width, width)],
@@ -50,6 +46,10 @@
              for i in range(pieces)]
     for load in sum(loads, []):
         load.start()
+    barrier = pltpu.get_barrier_semaphore()
+    for to in [partner] + [peers[d] for d in order]:
+        pl.semaphore_signal(barrier, inc=1, device_id={"rep": to}, device_id_type=MESH)
+
     state = [pltpu.make_async_copy(outer_params, params, state_sem.at[0]),
              pltpu.make_async_copy(momentum, speed, state_sem.at[1])]
     for load in state:

time: 23 us -> 23 us (level)
  no operation moved by 1% of the time
where the time goes in v4:
time: 23 us; the launch traced here: 22.9 us
  Pallas kernels  22.2 us (97%)
  between operations  0.64 us (3%)
    pallas_call x1, Pallas kernels, shards(): pl.pallas_call(functools.partial(exchange, n, chunks), out_shape=(pltpu.V...  20.3 us
    pallas_call x1, Pallas kernels, shards(): pl.pallas_call(functools.partial(finish, n), out_shape=(jax.ShapeDtypeStr...  1.89 us

profile of v4, /device:TPU:0, one launch (start us, length us, event | category | flops | bytes accessed | tf_op | source)
XLA Modules:
  0.0 22.9 jit_solution(10706524400657429071)
XLA Ops:
  0.6 20.3 %exchange.1 = (bf16[8,128,512]{2,1,0:T(8,128)(2,1)S(1)}, f32[128,512]{1,0:T(8,128)S(1)}, f32[128,512]{1,0:T(8,128)S(1)}) custom-call(s32[8]{0:T(128)} %presence.1, s32[8]{0:T(128)} %owner_of.3, bf16[1,128,4096]{2,1,0:T(8,128)(2,1)} %deltas.1, f32[128,512]{1,0:T(8,128)} %outer_params.1, f32[128,512]{1,0:T(8,128)} %momentum.1), custom_call_target="tpu_custom_call" | custom-call | tf_op jit(solution)/shard_map/exchange/pallas_call | solution.py:159
  21.0 1.9 %finish.1 = (bf16[128,4096]{1,0:T(8,128)(2,1)}, f32[128,512]{1,0:T(8,128)}, f32[128,512]{1,0:T(8,128)}) custom-call(s32[8]{0:T(128)} %owner_of.3, bf16[8,128,512]{2,1,0:T(8,128)(2,1)S(1)} %get-tuple-element.6.gathered, f32[128,512]{1,0:T(8,128)S(1)} %get-tuple-element.7.outer, f32[128,512]{1,0:T(8,128)S(1)} %get-tuple-element.8.speed), custom_call_target="tpu_custom_call" | custom-call | tf_op jit(solution)/shard_map/finish/pallas_call | solution.py:183
